TPU v7x, 256 devices: a whole 4x4x8 slice. The times are simulated.
256 devices in a mesh: stage: 32 (over z, y), expert: 8 (over x, core).
Axes of the slice: x: 4, y: 4, z: 8, core: 2. Of those that a mesh axis runs over, the one named last changes fastest.
Arguments:
- x_act: bfloat16 [32, 6144, 512], P('stage', 'expert')
- route_idx: int32 [32, 6144, 2], P('stage', 'expert')
- route_gate: float32 [32, 6144, 2], P('stage', 'expert')
- w_up: bfloat16 [32, 8, 512, 256], P('stage', 'expert')
- w_lin: bfloat16 [32, 8, 512, 256], P('stage', 'expert')
- w_down: bfloat16 [32, 8, 256, 512], P('stage', 'expert')
- dy_out: bfloat16 [32, 6144, 512], P('stage', 'expert')
Outputs:
- output 1: bfloat16 [32, 6144, 512], P('stage', 'expert')
- output 2: bfloat16 [32, 6144, 512], P('stage', 'expert')
- output 3: bfloat16 [32, 8, 512, 256], P('stage', 'expert')
- output 4: bfloat16 [32, 8, 512, 256], P('stage', 'expert')
- output 5: bfloat16 [32, 8, 256, 512], P('stage', 'expert')
All inputs are finite; a program needn't handle non-finite values.
Results may differ from a plain program's by a relative error of at most 0.001.
Values are sent between devices in bfloat16 or wider.
A program may use at most 768 MiB of HBM per device.

v0:
```python
import functools

import jax
import jax.numpy as jnp
from jax import lax
from jax.experimental import pallas as pl
from jax.experimental.pallas import tpu as pltpu
from jax.sharding import PartitionSpec as P

F32 = jnp.float32
BF16 = jnp.bfloat16
MESH = pl.DeviceIdType.MESH

OWN, SIB, LEFT, LEFT_SIB, RIGHT, RIGHT_SIB, OPP, OPP_SIB = range(8)


def cols(gate, width):
    return jnp.concatenate([gate] * (width // 128), axis=1)


def nt_dot(a, b):
    return lax.dot_general(a, b, (((1,), (1,)), ((), ())), preferred_element_type=F32)


def tn_dot(a, b):
    return lax.dot_general(a, b, (((0,), (0,)), ((), ())), preferred_element_type=F32)


def nn_dot(a, b):
    return jnp.dot(a, b, preferred_element_type=F32)


def expert_math(x_rows, dy_rows, gate, w_ul, w_down):
    ff = w_down.shape[0]
    routed = cols(gate, ff) > 0.0
    pre = nn_dot(x_rows, w_ul)
    pre_up = jnp.where(routed, pre[:, :ff], 0.0)
    pre_lin = jnp.where(routed, pre[:, ff:], 0.0)
    sig = 1.0 / (1.0 + jnp.exp(-pre_up))
    act = pre_up * sig
    hidden = (act * pre_lin).astype(BF16)
    u_rows = (cols(gate, dy_rows.shape[1]) * dy_rows.astype(F32)).astype(BF16)
    d_hid = nt_dot(u_rows, w_down).astype(BF16).astype(F32)
    d_up = (d_hid * pre_lin * sig * (1.0 + pre_up * (1.0 - sig))).astype(BF16)
    d_lin = (d_hid * act).astype(BF16)
    return hidden, u_rows, jnp.concatenate([d_up, d_lin], axis=1)


def moe_kernel(
    stages, groups, x_hbm, idx_hbm, gate_hbm, up_hbm, lin_hbm, down_hbm, dy_hbm,
    y_hbm, dx_hbm, dup_ref, dlin_ref, ddown_ref,
    w_all, d_all, x_all, idx_all, gate_all, gate_own, gate_exp, y_acc, dx_acc, y_buf, dx_buf, dul_acc, ddown_acc,
    load_sem, send_sem, recv_sem, small_send, small_recv, shift_send, shift_recv, out_sem,
):
    tokens, d_model = x_hbm.shape
    ff = down_hbm.shape[0]
    half, quarter = tokens // 2, tokens // 4
    stage, expert = lax.axis_index("stage"), lax.axis_index("expert")
    core = lax.rem(expert, 2)
    right = {"expert": lax.rem(expert + 2, groups)}
    left = {"expert": lax.rem(expert + groups - 2, groups)}
    sib = {"expert": expert + 1 - 2 * core}
    after = {"stage": lax.rem(stage + 1, stages)}
    before = {"stage": lax.rem(stage + stages - 1, stages)}

    loads = [
        pltpu.make_async_copy(up_hbm, w_all.at[OWN, pl.ds(0, d_model), pl.ds(0, ff)], load_sem.at[0]),
        pltpu.make_async_copy(lin_hbm, w_all.at[OWN, pl.ds(0, d_model), pl.ds(ff, ff)], load_sem.at[1]),
        pltpu.make_async_copy(down_hbm, w_all.at[OWN, pl.ds(d_model, ff)], load_sem.at[2]),
        pltpu.make_async_copy(dy_hbm, d_all.at[OWN], load_sem.at[3]),
    ]
    for load in loads:
        load.start()

    barrier = pltpu.get_barrier_semaphore()
    for peer in (right, left, sib, after, before):
        pl.semaphore_signal(barrier, inc=1, device_id=peer, device_id_type=MESH)
    pl.semaphore_wait(barrier, 5)

    started = []

    def remote(src, dst, send, recv, peer):
        return pltpu.make_async_remote_copy(src_ref=src, dst_ref=dst, send_sem=send, recv_sem=recv, device_id=peer, device_id_type=MESH)

    arrays = (w_all, d_all, x_all)
    kinds = [
        (OWN, LEFT, 0, half, right), (OWN, LEFT, half, half, right),
        (OWN, RIGHT, half, half, left), (OWN, RIGHT, 0, half, left),
        (OWN, SIB, 0, tokens, sib),
        (LEFT, OPP, 0, quarter, right), (LEFT, OPP, quarter, quarter, right),
        (RIGHT, OPP, half, quarter, left), (RIGHT, OPP, half + quarter, quarter, left),
        (LEFT, LEFT_SIB, 0, half, sib), (LEFT, LEFT_SIB, half, half, sib),
        (RIGHT, RIGHT_SIB, half, half, sib), (RIGHT, RIGHT_SIB, 0, half, sib),
        (OPP, OPP_SIB, 0, quarter, sib), (OPP, OPP_SIB, quarter, quarter, sib),
        (OPP, OPP_SIB, half, quarter, sib), (OPP, OPP_SIB, half + quarter, quarter, sib),
    ]

    def block_copy(array, kind):
        src_slot, dst_slot, row, rows, peer = kinds[kind]
        ref = arrays[array]
        return remote(
            ref.at[src_slot, pl.ds(row, rows)], ref.at[dst_slot, pl.ds(row, rows)],
            send_sem.at[array, kind], recv_sem.at[array, kind], peer,
        )

    def send(array, *which):
        for kind in which:
            copy = block_copy(array, kind)
            copy.start()
            started.append(copy)

    def arrive(array, *which):
        for kind in which:
            block_copy(array, kind).wait_recv()

    small = [(OWN, LEFT, right), (OWN, RIGHT, left), (OWN, SIB, sib), (LEFT, OPP, right), (LEFT, LEFT_SIB, sib), (RIGHT, RIGHT_SIB, sib), (OPP, OPP_SIB, sib)]

    def small_copies(kind):
        src_slot, dst_slot, peer = small[kind]
        return [
            remote(ref.at[src_slot], ref.at[dst_slot], small_send.at[which, kind], small_recv.at[which, kind], peer)
            for which, ref in enumerate((idx_all, gate_all))
        ]

    def send_small(*which):
        for kind in which:
            for copy in small_copies(kind):
                copy.start()
                started.append(copy)

    def arrive_small(*which):
        for kind in which:
            for copy in small_copies(kind):
                copy.wait_recv()

    shifts = [
        remote(idx_hbm, idx_all.at[OWN], shift_send.at[0], shift_recv.at[0], after),
        remote(gate_hbm, gate_all.at[OWN], shift_send.at[1], shift_recv.at[1], after),
        remote(x_hbm, x_all.at[OWN], shift_send.at[2], shift_recv.at[2], after),
    ]
    for copy in shifts:
        copy.start()
        started.append(copy)
    for load in loads:
        load.wait()
    send(0, 0, 2, 1, 3, 4)
    send(1, 0, 2, 1, 3, 4)

    def gate_columns(slot, expert_id):
        ids, gates = idx_all[slot], gate_all[slot]
        row = jnp.sum(jnp.where(ids == expert_id, gates, 0.0), axis=0, keepdims=True)
        return jnp.broadcast_to(row, (128, tokens)).T

    def expert_at(slot):
        chip_step = (0, 0, groups - 2, groups - 2, 2, 2, 4, 4)[slot]
        flip = (1 - 2 * core) if slot % 2 else 0
        return lax.rem(expert + flip + chip_step, groups)

    shifts[0].wait_recv()
    shifts[1].wait_recv()
    send_small(2, 0, 1)
    for slot in range(8):
        gate_own[slot] = gate_columns(OWN, expert_at(slot))
    gate_exp[OWN] = gate_columns(OWN, expert)
    y_acc[...] = jnp.zeros_like(y_acc)
    dx_acc[...] = jnp.zeros_like(dx_acc)
    dul_acc[...] = jnp.zeros_like(dul_acc)
    ddown_acc[...] = jnp.zeros_like(ddown_acc)
    arrive_small(2)
    gate_exp[SIB] = gate_columns(SIB, expert)

    def owner(first, last):
        def body(step, carry):
            slot = first + step // 2
            rows = pl.ds(pl.multiple_of(lax.rem(step, 2) * half, half), half)
            w_ul, w_down = w_all[slot, pl.ds(0, d_model)], w_all[slot, pl.ds(d_model, ff)]
            gate = gate_own[slot, rows]
            hidden, _, d_ul = expert_math(x_all[OWN, rows], d_all[OWN, rows], gate, w_ul, w_down)
            out = nn_dot(hidden, w_down).astype(BF16).astype(F32)
            y_acc[rows] += cols(gate, d_model) * out
            dx_acc[rows] += nt_dot(d_ul, w_ul).astype(BF16).astype(F32)
            return carry

        lax.fori_loop(0, 2 * (last - first), body, 0)

    def expert_rows(slot, rows):
        w_ul, w_down = w_all[OWN, pl.ds(0, d_model)], w_all[OWN, pl.ds(d_model, ff)]
        x_rows = x_all[slot, rows]
        hidden, u_rows, d_ul = expert_math(x_rows, d_all[slot, rows], gate_exp[slot, rows], w_ul, w_down)
        dul_acc[...] += tn_dot(x_rows, d_ul)
        ddown_acc[...] += tn_dot(hidden, u_rows)

    def expert_blocks(first, last):
        def body(step, carry):
            expert_rows(first + step // 2, pl.ds(pl.multiple_of(lax.rem(step, 2) * half, half), half))
            return carry

        lax.fori_loop(0, 2 * (last - first), body, 0)

    arrive(0, 0, 2)
    send(0, 5, 6, 7, 8, 9, 11)
    arrive(0, 1, 3)
    send(0, 10, 12)
    shifts[2].wait_recv()
    send(2, 4, 0, 2, 1, 3)
    arrive(0, 4)
    owner(OWN, LEFT)
    arrive(1, 0, 2)
    send(1, 5, 6, 7, 8, 9, 11)
    arrive(0, 9, 10, 11, 12)
    owner(LEFT, OPP)
    arrive(1, 1, 3)
    send(1, 10, 12)
    arrive(1, 4)
    arrive(2, 4)
    expert_blocks(OWN, LEFT)
    arrive(0, 5, 6, 7, 8)
    send(0, 13, 14, 15, 16)
    arrive_small(0, 1)
    send_small(3, 4, 5)
    arrive(0, 13, 14, 15, 16)
    owner(OPP, 8)
    y_buf[...] = y_acc[...].astype(BF16)
    dx_buf[...] = dx_acc[...].astype(BF16)
    gate_exp[LEFT] = gate_columns(LEFT, expert)
    gate_exp[RIGHT] = gate_columns(RIGHT, expert)
    arrive_small(3, 4, 5)
    send_small(6)
    gate_exp[LEFT_SIB] = gate_columns(LEFT_SIB, expert)
    gate_exp[RIGHT_SIB] = gate_columns(RIGHT_SIB, expert)
    gate_exp[OPP] = gate_columns(OPP, expert)
    back = remote(dx_buf, dx_hbm, shift_send.at[3], shift_recv.at[3], before)
    back.start()
    started.append(back)
    y_out = pltpu.make_async_copy(y_buf, y_hbm, out_sem.at[0])
    y_out.start()
    arrive(2, 0, 2)
    send(2, 5, 6, 7, 8, 9, 11)
    arrive_small(6)
    gate_exp[OPP_SIB] = gate_columns(OPP_SIB, expert)
    arrive(2, 1, 3)
    send(2, 10, 12)
    arrive(1, 9, 10, 11, 12)
    arrive(2, 9, 10, 11, 12)
    expert_blocks(LEFT, OPP)
    arrive(1, 5, 6, 7, 8)
    send(1, 13, 14, 15, 16)
    arrive(1, 13, 14, 15, 16)
    for part in range(2):
        arrive(2, 5 + part, 7 + part)
        send(2, 13 + part, 15 + part)

        def near(step, carry):
            expert_rows(OPP, pl.ds(pl.multiple_of(step * half + part * quarter, quarter), quarter))
            return carry

        def far(step, carry):
            expert_rows(OPP_SIB, pl.ds(pl.multiple_of(step * half + part * quarter, quarter), quarter))
            return carry

        lax.fori_loop(0, 2, near, 0)
        arrive(2, 13 + part, 15 + part)
        lax.fori_loop(0, 2, far, 0)

    dup_ref[...] = dul_acc[:, :ff].astype(BF16)
    dlin_ref[...] = dul_acc[:, ff:].astype(BF16)
    ddown_ref[...] = ddown_acc[...].astype(BF16)
    for copy in started:
        copy.wait_send()
    back.wait_recv()
    y_out.wait()


def solution(mesh):
    stages = mesh.shape["stage"]
    groups = mesh.shape["expert"]
    tok_spec = P("stage", "expert", None)
    w_spec = P("stage", "expert", None, None)

    def device_step(x_act, route_idx, route_gate, w_up, w_lin, w_down, dy_out):
        _, tokens, d_model = x_act.shape
        ff = w_up.shape[-1]
        any_spec = pl.BlockSpec(memory_space=pl.ANY)
        vmem_spec = pl.BlockSpec(memory_space=pltpu.VMEM)
        dma = pltpu.SemaphoreType.DMA
        y_tok, dx_prev, g_up, g_lin, g_down = pl.pallas_call(
            functools.partial(moe_kernel, stages, groups),
            name="moe",
            out_shape=(
                jax.ShapeDtypeStruct((tokens, d_model), BF16),
                jax.ShapeDtypeStruct((tokens, d_model), BF16),
                jax.ShapeDtypeStruct((d_model, ff), BF16),
                jax.ShapeDtypeStruct((d_model, ff), BF16),
                jax.ShapeDtypeStruct((ff, d_model), BF16),
            ),
            in_specs=[any_spec] * 7,
            out_specs=(any_spec, any_spec, vmem_spec, vmem_spec, vmem_spec),
            scratch_shapes=[
                pltpu.VMEM((8, d_model + ff, d_model), BF16),
                pltpu.VMEM((8, tokens, d_model), BF16),
                pltpu.VMEM((8, tokens, d_model), BF16),
                pltpu.VMEM((8, 2, tokens), jnp.int32),
                pltpu.VMEM((8, 2, tokens), F32),
                pltpu.VMEM((8, tokens, 128), F32),
                pltpu.VMEM((8, tokens, 128), F32),
                pltpu.VMEM((tokens, d_model), F32),
                pltpu.VMEM((tokens, d_model), F32),
                pltpu.VMEM((tokens, d_model), BF16),
                pltpu.VMEM((tokens, d_model), BF16),
                pltpu.VMEM((d_model, 2 * ff), F32),
                pltpu.VMEM((ff, d_model), F32),
                dma((4,)),
                dma((3, 17)),
                dma((3, 17)),
                dma((2, 7)),
                dma((2, 7)),
                dma((4,)),
                dma((4,)),
                dma((1,)),
            ],
            compiler_params=pltpu.CompilerParams(collective_id=0, has_side_effects=True, vmem_limit_bytes=60 * 1024 * 1024),
        )(x_act[0], route_idx[0].T, route_gate[0].T, w_up[0, 0], w_lin[0, 0], w_down[0, 0], dy_out[0])
        return y_tok[None], dx_prev[None], g_up[None, None], g_lin[None, None], g_down[None, None]

    return jax.shard_map(device_step, mesh=mesh, in_specs=(tok_spec, tok_spec, tok_spec, w_spec, w_spec, w_spec, tok_spec), out_specs=(tok_spec, tok_spec, w_spec, w_spec, w_spec), check_vma=False)
```

profile of v0, /device:TPU:1, one launch (start us, length us, event | category | flops | bytes accessed | tf_op | source)
XLA Modules:
  0.0 112.0 jit_solution(5119332171783709231)
XLA Ops:
  0.6 105.3 %moe.1 = (bf16[768,512]{1,0:T(8,128)(2,1)}, bf16[768,512]{1,0:T(8,128)(2,1)}, bf16[512,256]{1,0:T(8,128)(2,1)}, bf16[512,256]{1,0:T(8,128)(2,1)}, bf16[256,512]{1,0:T(8,128)(2,1)}) custom-call(bf16[768,512]{1,0:T(8,128)(2,1)} %bitcast.18, s32[2,768]{1,0:T(2,128)} %bitcast.26, f32[2,768]{1,0:T(2,128)} %bitcast.27, bf16[512,256]{1,0:T(8,128)(2,1)} %bitcast.20, ...), custom_call_target="tpu_custom_call" | custom-call | tf_op jit(solution)/shard_map/moe/pallas_call | solution.py:286
  106.0 0.0 copy-start
  106.0 2.1 %copy.17 = bf16[1,768,512]{2,1,0:T(8,128)(2,1)} copy(bf16[1,768,512]{2,1,0:T(8,128)(2,1)} %bitcast.17) | data formatting | bytes 1572864
  108.1 0.0 copy-done
  108.1 0.0 copy-start.3
  108.1 0.9 copy.18
  109.0 0.2 copy-done.3
  109.2 0.0 copy-start.2
  109.2 0.7 copy.19
  109.9 0.3 copy-done.2
  110.3 0.0 copy-start.1
  110.3 0.7 copy.20
  111.0 0.3 copy-done.1
  111.3 0.7 copy.21
Async XLA Ops:
  106.0 2.1 %copy-start = (bf16[768,512]{1,0:T(8,128)(2,1)S(1)}, bf16[768,512]{1,0:T(8,128)(2,1)}, u32[]{:S(2)}) copy-start(bf16[768,512]{1,0:T(8,128)(2,1)} %get-tuple-element.11) | copy-start | bytes 2359300
  108.1 1.1 copy-start.3
  109.2 1.0 copy-start.2
  110.3 1.0 copy-start.1
where the time goes:
time: 112 us
  Pallas kernels  105 us (94%)
  local copies, waits for them, and re-layouts  6.02 us (5%)
    pallas_call x1, Pallas kernels, device_step(): pl.pallas_call(functools.partial(moe_kernel, stages, groups), name='moe',...  105 us
    unnamed x13, local copies, waits for them, and re-layouts  6.02 us

commit v1 on v0

--- a/solution.py
+++ b/solution.py
@@ -48,13 +48,14 @@
 
 def moe_kernel(
     stages, groups, x_hbm, idx_hbm, gate_hbm, up_hbm, lin_hbm, down_hbm, dy_hbm,
-    y_hbm, dx_hbm, dup_ref, dlin_ref, ddown_ref,
-    w_all, d_all, x_all, idx_all, gate_all, gate_own, gate_exp, y_acc, dx_acc, y_buf, dx_buf, dul_acc, ddown_acc,
-    load_sem, send_sem, recv_sem, small_send, small_recv, shift_send, shift_recv, out_sem,
+    y_ref, dx_ref, dup_ref, dlin_ref, ddown_ref,
+    w_all, d_all, x_all, idx_all, gate_all, gate_own, gate_exp, y_acc, dx_acc, dx_buf, dul_acc, ddown_acc,
+    load_sem, send_sem, recv_sem, small_send, small_recv, shift_send, shift_recv,
 ):
     tokens, d_model = x_hbm.shape
     ff = down_hbm.shape[0]
-    half, quarter = tokens // 2, tokens // 4
+    half, cut = tokens // 2, 3 * tokens // 8
+    rest = half - cut
     stage, expert = lax.axis_index("stage"), lax.axis_index("expert")
     core = lax.rem(expert, 2)
     right = {"expert": lax.rem(expert + 2, groups)}
@@ -87,12 +88,12 @@
         (OWN, LEFT, 0, half, right), (OWN, LEFT, half, half, right),
         (OWN, RIGHT, half, half, left), (OWN, RIGHT, 0, half, left),
         (OWN, SIB, 0, tokens, sib),
-        (LEFT, OPP, 0, quarter, right), (LEFT, OPP, quarter, quarter, right),
-        (RIGHT, OPP, half, quarter, left), (RIGHT, OPP, half + quarter, quarter, left),
+        (LEFT, OPP, 0, cut, right), (LEFT, OPP, cut, rest, right),
+        (RIGHT, OPP, tokens - cut, cut, left), (RIGHT, OPP, half, rest, left),
         (LEFT, LEFT_SIB, 0, half, sib), (LEFT, LEFT_SIB, half, half, sib),
         (RIGHT, RIGHT_SIB, half, half, sib), (RIGHT, RIGHT_SIB, 0, half, sib),
-        (OPP, OPP_SIB, 0, quarter, sib), (OPP, OPP_SIB, quarter, quarter, sib),
-        (OPP, OPP_SIB, half, quarter, sib), (OPP, OPP_SIB, half + quarter, quarter, sib),
+        (OPP, OPP_SIB, 0, cut, sib), (OPP, OPP_SIB, cut, rest, sib),
+        (OPP, OPP_SIB, tokens - cut, cut, sib), (OPP, OPP_SIB, half, rest, sib),
     ]
 
     def block_copy(array, kind):
@@ -144,7 +145,6 @@
     for load in loads:
         load.wait()
     send(0, 0, 2, 1, 3, 4)
-    send(1, 0, 2, 1, 3, 4)
 
     def gate_columns(slot, expert_id):
         ids, gates = idx_all[slot], gate_all[slot]
@@ -159,6 +159,7 @@
     shifts[0].wait_recv()
     shifts[1].wait_recv()
     send_small(2, 0, 1)
+    send(1, 0, 2, 1, 3, 4)
     for slot in range(8):
         gate_own[slot] = gate_columns(OWN, expert_at(slot))
     gate_exp[OWN] = gate_columns(OWN, expert)
@@ -199,6 +200,10 @@
 
     arrive(0, 0, 2)
     send(0, 5, 6, 7, 8, 9, 11)
+    arrive_small(0, 1)
+    send_small(3, 4, 5)
+    gate_exp[LEFT] = gate_columns(LEFT, expert)
+    gate_exp[RIGHT] = gate_columns(RIGHT, expert)
     arrive(0, 1, 3)
     send(0, 10, 12)
     shifts[2].wait_recv()
@@ -211,33 +216,27 @@
     owner(LEFT, OPP)
     arrive(1, 1, 3)
     send(1, 10, 12)
+    arrive_small(3, 4, 5)
+    send_small(6)
+    gate_exp[LEFT_SIB] = gate_columns(LEFT_SIB, expert)
+    gate_exp[RIGHT_SIB] = gate_columns(RIGHT_SIB, expert)
+    gate_exp[OPP] = gate_columns(OPP, expert)
     arrive(1, 4)
     arrive(2, 4)
     expert_blocks(OWN, LEFT)
     arrive(0, 5, 6, 7, 8)
     send(0, 13, 14, 15, 16)
-    arrive_small(0, 1)
-    send_small(3, 4, 5)
+    arrive_small(6)
+    gate_exp[OPP_SIB] = gate_columns(OPP_SIB, expert)
     arrive(0, 13, 14, 15, 16)
     owner(OPP, 8)
-    y_buf[...] = y_acc[...].astype(BF16)
+    y_ref[...] = y_acc[...].astype(BF16)
     dx_buf[...] = dx_acc[...].astype(BF16)
-    gate_exp[LEFT] = gate_columns(LEFT, expert)
-    gate_exp[RIGHT] = gate_columns(RIGHT, expert)
-    arrive_small(3, 4, 5)
-    send_small(6)
-    gate_exp[LEFT_SIB] = gate_columns(LEFT_SIB, expert)
-    gate_exp[RIGHT_SIB] = gate_columns(RIGHT_SIB, expert)
-    gate_exp[OPP] = gate_columns(OPP, expert)
-    back = remote(dx_buf, dx_hbm, shift_send.at[3], shift_recv.at[3], before)
+    arrive(2, 0, 2)
+    send(2, 5, 6, 7, 8, 9, 11)
+    back = remote(dx_buf, dx_ref, shift_send.at[3], shift_recv.at[3], before)
     back.start()
     started.append(back)
-    y_out = pltpu.make_async_copy(y_buf, y_hbm, out_sem.at[0])
-    y_out.start()
-    arrive(2, 0, 2)
-    send(2, 5, 6, 7, 8, 9, 11)
-    arrive_small(6)
-    gate_exp[OPP_SIB] = gate_columns(OPP_SIB, expert)
     arrive(2, 1, 3)
     send(2, 10, 12)
     arrive(1, 9, 10, 11, 12)
@@ -245,22 +244,25 @@
     expert_blocks(LEFT, OPP)
     arrive(1, 5, 6, 7, 8)
     send(1, 13, 14, 15, 16)
+    arrive(2, 5, 7)
+    send(2, 13, 15)
+
+    def outer(slot):
+        def body(step, carry):
+            expert_rows(slot, pl.ds(pl.multiple_of(step * (tokens - cut), 32), cut))
+            return carry
+
+        lax.fori_loop(0, 2, body, 0)
+
+    outer(OPP)
     arrive(1, 13, 14, 15, 16)
-    for part in range(2):
-        arrive(2, 5 + part, 7 + part)
-        send(2, 13 + part, 15 + part)
-
-        def near(step, carry):
-            expert_rows(OPP, pl.ds(pl.multiple_of(step * half + part * quarter, quarter), quarter))
-            return carry
-
-        def far(step, carry):
-            expert_rows(OPP_SIB, pl.ds(pl.multiple_of(step * half + part * quarter, quarter), quarter))
-            return carry
-
-        lax.fori_loop(0, 2, near, 0)
-        arrive(2, 13 + part, 15 + part)
-        lax.fori_loop(0, 2, far, 0)
+    arrive(2, 13, 15)
+    outer(OPP_SIB)
+    arrive(2, 6, 8)
+    send(2, 14, 16)
+    expert_rows(OPP, pl.ds(cut, 2 * rest))
+    arrive(2, 14, 16)
+    expert_rows(OPP_SIB, pl.ds(cut, 2 * rest))
 
     dup_ref[...] = dul_acc[:, :ff].astype(BF16)
     dlin_ref[...] = dul_acc[:, ff:].astype(BF16)
@@ -268,7 +270,15 @@
     for copy in started:
         copy.wait_send()
     back.wait_recv()
-    y_out.wait()
+
+
+def finish_kernel(*refs):
+    count = len(refs) // 2
+    outs = [pltpu.make_async_copy(refs[i], refs[count + i], refs[-1].at[i]) for i in range(count)]
+    for copy in outs:
+        copy.start()
+    for copy in outs:
+        copy.wait()
 
 
 def solution(mesh):
@@ -283,18 +293,18 @@
         any_spec = pl.BlockSpec(memory_space=pl.ANY)
         vmem_spec = pl.BlockSpec(memory_space=pltpu.VMEM)
         dma = pltpu.SemaphoreType.DMA
-        y_tok, dx_prev, g_up, g_lin, g_down = pl.pallas_call(
+        results = pl.pallas_call(
             functools.partial(moe_kernel, stages, groups),
             name="moe",
             out_shape=(
-                jax.ShapeDtypeStruct((tokens, d_model), BF16),
-                jax.ShapeDtypeStruct((tokens, d_model), BF16),
-                jax.ShapeDtypeStruct((d_model, ff), BF16),
-                jax.ShapeDtypeStruct((d_model, ff), BF16),
-                jax.ShapeDtypeStruct((ff, d_model), BF16),
+                pltpu.VMEM((tokens, d_model), BF16),
+                pltpu.VMEM((tokens, d_model), BF16),
+                pltpu.VMEM((d_model, ff), BF16),
+                pltpu.VMEM((d_model, ff), BF16),
+                pltpu.VMEM((ff, d_model), BF16),
             ),
             in_specs=[any_spec] * 7,
-            out_specs=(any_spec, any_spec, vmem_spec, vmem_spec, vmem_spec),
+            out_specs=(vmem_spec,) * 5,
             scratch_shapes=[
                 pltpu.VMEM((8, d_model + ff, d_model), BF16),
                 pltpu.VMEM((8, tokens, d_model), BF16),
@@ -306,7 +316,6 @@
                 pltpu.VMEM((tokens, d_model), F32),
                 pltpu.VMEM((tokens, d_model), F32),
                 pltpu.VMEM((tokens, d_model), BF16),
-                pltpu.VMEM((tokens, d_model), BF16),
                 pltpu.VMEM((d_model, 2 * ff), F32),
                 pltpu.VMEM((ff, d_model), F32),
                 dma((4,)),
@@ -316,10 +325,18 @@
                 dma((2, 7)),
                 dma((4,)),
                 dma((4,)),
-                dma((1,)),
             ],
             compiler_params=pltpu.CompilerParams(collective_id=0, has_side_effects=True, vmem_limit_bytes=60 * 1024 * 1024),
         )(x_act[0], route_idx[0].T, route_gate[0].T, w_up[0, 0], w_lin[0, 0], w_down[0, 0], dy_out[0])
+        shapes = [jax.ShapeDtypeStruct(r.shape, r.dtype) for r in results]
+        y_tok, dx_prev, g_up, g_lin, g_down = pl.pallas_call(
+            finish_kernel,
+            name="finish",
+            out_shape=shapes,
+            in_specs=[vmem_spec] * 5,
+            out_specs=[any_spec] * 5,
+            scratch_shapes=[dma((5,))],
+        )(*[pltpu.with_memory_space_constraint(r, pltpu.VMEM) for r in results])
         return y_tok[None], dx_prev[None], g_up[None, None], g_lin[None, None], g_down[None, None]
 
     return jax.shard_map(device_step, mesh=mesh, in_specs=(tok_spec, tok_spec, tok_spec, w_spec, w_spec, w_spec, tok_spec), out_specs=(tok_spec, tok_spec, w_spec, w_spec, w_spec), check_vma=False)

time: 112 us -> 98.2 us (0.88)
  Pallas kernels: 105 us -> 97.5 us
  local copies, waits for them, and re-layouts: 6.02 us -> 0 us
    pallas_call x1, Pallas kernels: 105 us -> 96.1 us  [device_step(): pl.pallas_call(functools.partial(moe_kernel, stages, groups), name='moe',...]
    unnamed x13 -> x0, local copies, waits for them, and re-layouts: 6.02 us -> none
    pallas_call x0 -> x1, Pallas kernels: none -> 1.44 us  [device_step(): pl.pallas_call(finish_kernel, name='finish', out_shape=shapes, in_specs=[...]
where the time goes in v1:
time: 98.2 us; the launch traced here: 98.1 us
  Pallas kernels  97.5 us (99%)
    pallas_call x1, Pallas kernels, device_step(): pl.pallas_call(functools.partial(moe_kernel, stages, groups), name='moe',...  96.1 us

profile of v1, /device:TPU:1, one launch (start us, length us, event | category | flops | bytes accessed | tf_op | source)
XLA Modules:
  0.0 98.1 jit_solution(247366805237009333)
XLA Ops:
  0.6 96.1 %moe.1 = (bf16[768,512]{1,0:T(8,128)(2,1)S(1)}, bf16[768,512]{1,0:T(8,128)(2,1)S(1)}, bf16[512,256]{1,0:T(8,128)(2,1)S(1)}, bf16[512,256]{1,0:T(8,128)(2,1)S(1)}, bf16[256,512]{1,0:T(8,128)(2,1)S(1)}) custom-call(bf16[768,512]{1,0:T(8,128)(2,1)} %bitcast.16, s32[2,768]{1,0:T(2,128)} %bitcast.21, f32[2,768]{1,0:T(2,128)} %bitcast.22, ...), custom_call_target="tpu_custom_call" | custom-call | tf_op jit(solution)/shard_map/moe/pallas_call | solution.py:296
  96.7 1.4 %finish.1 = (bf16[768,512]{1,0:T(8,128)(2,1)}, bf16[768,512]{1,0:T(8,128)(2,1)}, bf16[512,256]{1,0:T(8,128)(2,1)}, bf16[512,256]{1,0:T(8,128)(2,1)}, bf16[256,512]{1,0:T(8,128)(2,1)}) custom-call(bf16[768,512]{1,0:T(8,128)(2,1)S(1)} %get-tuple-element.15.refs_0_, bf16[768,512]{1,0:T(8,128)(2,1)S(1)} %get-tuple-element.16.refs_1_, ...), custom_call_target="tpu_custom_call" | custom-call | tf_op jit(solution)/shard_map/finish/pallas_call | solution.py:332

commit v2 on v1

--- a/solution.py
+++ b/solution.py
@@ -50,7 +50,7 @@
     stages, groups, x_hbm, idx_hbm, gate_hbm, up_hbm, lin_hbm, down_hbm, dy_hbm,
     y_ref, dx_ref, dup_ref, dlin_ref, ddown_ref,
     w_all, d_all, x_all, idx_all, gate_all, gate_own, gate_exp, y_acc, dx_acc, dx_buf, dul_acc, ddown_acc,
-    load_sem, send_sem, recv_sem, small_send, small_recv, shift_send, shift_recv,
+    load_sem, send_sem, recv_sem, small_send, small_recv, shift_send, shift_recv, ring_ready, stage_ready, sib_ready,
 ):
     tokens, d_model = x_hbm.shape
     ff = down_hbm.shape[0]
@@ -74,9 +74,24 @@
         load.start()
 
     barrier = pltpu.get_barrier_semaphore()
-    for peer in (right, left, sib, after, before):
-        pl.semaphore_signal(barrier, inc=1, device_id=peer, device_id_type=MESH)
-    pl.semaphore_wait(barrier, 5)
+    colour = lax.rem(expert // 2 + core, 2)
+
+    def signal(sem, *peers):
+        for peer in peers:
+            pl.semaphore_signal(sem, inc=1, device_id=peer, device_id_type=MESH)
+
+    @pl.when(colour == 1)
+    def _():
+        signal(barrier, right, left, sib, after, before)
+
+    @pl.when(colour == 0)
+    def _():
+        pl.semaphore_wait(barrier, 3)
+        signal(ring_ready, right, left, sib)
+
+    @pl.when(colour == 1)
+    def _():
+        pl.semaphore_wait(ring_ready, 3)
 
     started = []
 
@@ -134,6 +149,21 @@
             for copy in small_copies(kind):
                 copy.wait_recv()
 
+    for load in loads:
+        load.wait()
+    send(0, 0, 2, 1, 3, 4)
+
+    @pl.when(colour == 1)
+    def _():
+        pl.semaphore_wait(barrier, 2)
+        signal(stage_ready, after, before)
+        pl.semaphore_wait(stage_ready, 2)
+        signal(sib_ready, sib)
+
+    @pl.when(colour == 0)
+    def _():
+        pl.semaphore_wait(sib_ready, 1)
+
     shifts = [
         remote(idx_hbm, idx_all.at[OWN], shift_send.at[0], shift_recv.at[0], after),
         remote(gate_hbm, gate_all.at[OWN], shift_send.at[1], shift_recv.at[1], after),
@@ -142,9 +172,6 @@
     for copy in shifts:
         copy.start()
         started.append(copy)
-    for load in loads:
-        load.wait()
-    send(0, 0, 2, 1, 3, 4)
 
     def gate_columns(slot, expert_id):
         ids, gates = idx_all[slot], gate_all[slot]
@@ -325,6 +352,9 @@
                 dma((2, 7)),
                 dma((4,)),
                 dma((4,)),
+                pltpu.SemaphoreType.REGULAR,
+                pltpu.SemaphoreType.REGULAR,
+                pltpu.SemaphoreType.REGULAR,
             ],
             compiler_params=pltpu.CompilerParams(collective_id=0, has_side_effects=True, vmem_limit_bytes=60 * 1024 * 1024),
         )(x_act[0], route_idx[0].T, route_gate[0].T, w_up[0, 0], w_lin[0, 0], w_down[0, 0], dy_out[0])

time: 98.2 us -> 91.6 us (0.933)
  Pallas kernels: 97.5 us -> 90.8 us
    pallas_call x1, Pallas kernels: 96.1 us -> 89.4 us  [device_step(): pl.pallas_call(functools.partial(moe_kernel, stages, groups), name='moe',...]
where the time goes in v2:
time: 91.6 us; the launch traced here: 91.5 us
  Pallas kernels  90.8 us (99%)
    pallas_call x1, Pallas kernels, device_step(): pl.pallas_call(functools.partial(moe_kernel, stages, groups), name='moe',...  89.4 us

profile of v2, /device:TPU:1, one launch (start us, length us, event | category | flops | bytes accessed | tf_op | source)
XLA Modules:
  0.0 91.5 jit_solution(17056630748099114062)
XLA Ops:
  0.6 89.4 %moe.1 = (bf16[768,512]{1,0:T(8,128)(2,1)S(1)}, bf16[768,512]{1,0:T(8,128)(2,1)S(1)}, bf16[512,256]{1,0:T(8,128)(2,1)S(1)}, bf16[512,256]{1,0:T(8,128)(2,1)S(1)}, bf16[256,512]{1,0:T(8,128)(2,1)S(1)}) custom-call(bf16[768,512]{1,0:T(8,128)(2,1)} %bitcast.16, s32[2,768]{1,0:T(2,128)} %bitcast.21, f32[2,768]{1,0:T(2,128)} %bitcast.22, ...), custom_call_target="tpu_custom_call" | custom-call | tf_op jit(solution)/shard_map/moe/pallas_call | solution.py:323
  90.0 1.4 %finish.1 = (bf16[768,512]{1,0:T(8,128)(2,1)}, bf16[768,512]{1,0:T(8,128)(2,1)}, bf16[512,256]{1,0:T(8,128)(2,1)}, bf16[512,256]{1,0:T(8,128)(2,1)}, bf16[256,512]{1,0:T(8,128)(2,1)}) custom-call(bf16[768,512]{1,0:T(8,128)(2,1)S(1)} %get-tuple-element.15.refs_0_, bf16[768,512]{1,0:T(8,128)(2,1)S(1)} %get-tuple-element.16.refs_1_, ...), custom_call_target="tpu_custom_call" | custom-call | tf_op jit(solution)/shard_map/finish/pallas_call | solution.py:362

commit v3 on v2

--- a/solution.py
+++ b/solution.py
@@ -30,7 +30,12 @@
     return jnp.dot(a, b, preferred_element_type=F32)
 
 
-def expert_math(x_rows, dy_rows, gate, w_ul, w_down):
+def hidden_cotangent(dy_rows, gate, w_down):
+    u_rows = (cols(gate, dy_rows.shape[1]) * dy_rows.astype(F32)).astype(BF16)
+    return u_rows, nt_dot(u_rows, w_down).astype(BF16)
+
+
+def expert_math(x_rows, dy_rows, gate, w_ul, w_down, ready=None):
     ff = w_down.shape[0]
     routed = cols(gate, ff) > 0.0
     pre = nn_dot(x_rows, w_ul)
@@ -39,8 +44,8 @@
     sig = 1.0 / (1.0 + jnp.exp(-pre_up))
     act = pre_up * sig
     hidden = (act * pre_lin).astype(BF16)
-    u_rows = (cols(gate, dy_rows.shape[1]) * dy_rows.astype(F32)).astype(BF16)
-    d_hid = nt_dot(u_rows, w_down).astype(BF16).astype(F32)
+    u_rows, d_hid = hidden_cotangent(dy_rows, gate, w_down) if ready is None else ready
+    d_hid = d_hid.astype(F32)
     d_up = (d_hid * pre_lin * sig * (1.0 + pre_up * (1.0 - sig))).astype(BF16)
     d_lin = (d_hid * act).astype(BF16)
     return hidden, u_rows, jnp.concatenate([d_up, d_lin], axis=1)
@@ -49,7 +54,7 @@
 def moe_kernel(
     stages, groups, x_hbm, idx_hbm, gate_hbm, up_hbm, lin_hbm, down_hbm, dy_hbm,
     y_ref, dx_ref, dup_ref, dlin_ref, ddown_ref,
-    w_all, d_all, x_all, idx_all, gate_all, gate_own, gate_exp, y_acc, dx_acc, dx_buf, dul_acc, ddown_acc,
+    w_all, d_all, x_all, idx_all, gate_all, gate_own, gate_exp, y_acc, dx_acc, dx_buf, dul_acc, ddown_acc, u_opp, dh_opp,
     load_sem, send_sem, recv_sem, small_send, small_recv, shift_send, shift_recv, ring_ready, stage_ready, sib_ready,
 ):
     tokens, d_model = x_hbm.shape
@@ -211,19 +216,19 @@
 
         lax.fori_loop(0, 2 * (last - first), body, 0)
 
-    def expert_rows(slot, rows):
+    def expert_rows(slot, rows, ready=None):
         w_ul, w_down = w_all[OWN, pl.ds(0, d_model)], w_all[OWN, pl.ds(d_model, ff)]
         x_rows = x_all[slot, rows]
-        hidden, u_rows, d_ul = expert_math(x_rows, d_all[slot, rows], gate_exp[slot, rows], w_ul, w_down)
+        hidden, u_rows, d_ul = expert_math(x_rows, d_all[slot, rows], gate_exp[slot, rows], w_ul, w_down, ready)
         dul_acc[...] += tn_dot(x_rows, d_ul)
         ddown_acc[...] += tn_dot(hidden, u_rows)
 
-    def expert_blocks(first, last):
+    def expert_blocks(first, stride):
         def body(step, carry):
-            expert_rows(first + step // 2, pl.ds(pl.multiple_of(lax.rem(step, 2) * half, half), half))
+            expert_rows(first + step * stride, pl.ds(0, tokens))
             return carry
 
-        lax.fori_loop(0, 2 * (last - first), body, 0)
+        lax.fori_loop(0, 2, body, 0)
 
     arrive(0, 0, 2)
     send(0, 5, 6, 7, 8, 9, 11)
@@ -250,7 +255,7 @@
     gate_exp[OPP] = gate_columns(OPP, expert)
     arrive(1, 4)
     arrive(2, 4)
-    expert_blocks(OWN, LEFT)
+    expert_blocks(OWN, 1)
     arrive(0, 5, 6, 7, 8)
     send(0, 13, 14, 15, 16)
     arrive_small(6)
@@ -266,30 +271,28 @@
     started.append(back)
     arrive(2, 1, 3)
     send(2, 10, 12)
+    expert_blocks(LEFT, 2)
     arrive(1, 9, 10, 11, 12)
     arrive(2, 9, 10, 11, 12)
-    expert_blocks(LEFT, OPP)
+    expert_blocks(LEFT_SIB, 2)
     arrive(1, 5, 6, 7, 8)
     send(1, 13, 14, 15, 16)
+
+    def prepare(slot):
+        u_rows, d_hid = hidden_cotangent(d_all[slot], gate_exp[slot], w_all[OWN, pl.ds(d_model, ff)])
+        u_opp[slot - OPP] = u_rows
+        dh_opp[slot - OPP] = d_hid
+
+    prepare(OPP)
+    arrive(1, 13, 14, 15, 16)
+    prepare(OPP_SIB)
     arrive(2, 5, 7)
     send(2, 13, 15)
-
-    def outer(slot):
-        def body(step, carry):
-            expert_rows(slot, pl.ds(pl.multiple_of(step * (tokens - cut), 32), cut))
-            return carry
-
-        lax.fori_loop(0, 2, body, 0)
-
-    outer(OPP)
-    arrive(1, 13, 14, 15, 16)
-    arrive(2, 13, 15)
-    outer(OPP_SIB)
     arrive(2, 6, 8)
     send(2, 14, 16)
-    expert_rows(OPP, pl.ds(cut, 2 * rest))
-    arrive(2, 14, 16)
-    expert_rows(OPP_SIB, pl.ds(cut, 2 * rest))
+    expert_rows(OPP, pl.ds(0, tokens), (u_opp[0], dh_opp[0]))
+    arrive(2, 13, 14, 15, 16)
+    expert_rows(OPP_SIB, pl.ds(0, tokens), (u_opp[1], dh_opp[1]))
 
     dup_ref[...] = dul_acc[:, :ff].astype(BF16)
     dlin_ref[...] = dul_acc[:, ff:].astype(BF16)
@@ -345,6 +348,8 @@
                 pltpu.VMEM((tokens, d_model), BF16),
                 pltpu.VMEM((d_model, 2 * ff), F32),
                 pltpu.VMEM((ff, d_model), F32),
+                pltpu.VMEM((2, tokens, d_model), BF16),
+                pltpu.VMEM((2, tokens, ff), BF16),
                 dma((4,)),
                 dma((3, 17)),
                 dma((3, 17)),

time: 91.6 us -> 88.6 us (0.967)
  Pallas kernels: 90.8 us -> 87.9 us
    pallas_call x1, Pallas kernels: 89.4 us -> 86.4 us  [device_step(): pl.pallas_call(functools.partial(moe_kernel, stages, groups), name='moe',...]
where the time goes in v3:
time: 88.6 us; the launch traced here: 88.5 us
  Pallas kernels  87.9 us (99%)
    pallas_call x1, Pallas kernels, device_step(): pl.pallas_call(functools.partial(moe_kernel, stages, groups), name='moe',...  86.4 us

profile of v3, /device:TPU:1, one launch (start us, length us, event | category | flops | bytes accessed | tf_op | source)
XLA Modules:
  0.0 88.5 jit_solution(2607089727709257345)
XLA Ops:
  0.6 86.4 %moe.1 = (bf16[768,512]{1,0:T(8,128)(2,1)S(1)}, bf16[768,512]{1,0:T(8,128)(2,1)S(1)}, bf16[512,256]{1,0:T(8,128)(2,1)S(1)}, bf16[512,256]{1,0:T(8,128)(2,1)S(1)}, bf16[256,512]{1,0:T(8,128)(2,1)S(1)}) custom-call(bf16[768,512]{1,0:T(8,128)(2,1)} %bitcast.16, s32[2,768]{1,0:T(2,128)} %bitcast.21, f32[2,768]{1,0:T(2,128)} %bitcast.22, ...), custom_call_target="tpu_custom_call" | custom-call | tf_op jit(solution)/shard_map/moe/pallas_call | solution.py:326
  87.1 1.4 %finish.1 = (bf16[768,512]{1,0:T(8,128)(2,1)}, bf16[768,512]{1,0:T(8,128)(2,1)}, bf16[512,256]{1,0:T(8,128)(2,1)}, bf16[512,256]{1,0:T(8,128)(2,1)}, bf16[256,512]{1,0:T(8,128)(2,1)}) custom-call(bf16[768,512]{1,0:T(8,128)(2,1)S(1)} %get-tuple-element.15.refs_0_, bf16[768,512]{1,0:T(8,128)(2,1)S(1)} %get-tuple-element.16.refs_1_, ...), custom_call_target="tpu_custom_call" | custom-call | tf_op jit(solution)/shard_map/finish/pallas_call | solution.py:367

commit v4 on v3

--- a/solution.py
+++ b/solution.py
@@ -75,7 +75,7 @@
         pltpu.make_async_copy(down_hbm, w_all.at[OWN, pl.ds(d_model, ff)], load_sem.at[2]),
         pltpu.make_async_copy(dy_hbm, d_all.at[OWN], load_sem.at[3]),
     ]
-    for load in loads:
+    for load in loads[:3]:
         load.start()
 
     barrier = pltpu.get_barrier_semaphore()
@@ -137,11 +137,11 @@
     small = [(OWN, LEFT, right), (OWN, RIGHT, left), (OWN, SIB, sib), (LEFT, OPP, right), (LEFT, LEFT_SIB, sib), (RIGHT, RIGHT_SIB, sib), (OPP, OPP_SIB, sib)]
 
     def small_copies(kind):
-        src_slot, dst_slot, peer = small[kind]
-        return [
-            remote(ref.at[src_slot], ref.at[dst_slot], small_send.at[which, kind], small_recv.at[which, kind], peer)
-            for which, ref in enumerate((idx_all, gate_all))
-        ]
+        copies = []
+        for which, ref in enumerate((idx_all, gate_all)):
+            src_slot, dst_slot, peer = (RIGHT, OPP, left) if (kind, which) == (3, 1) else small[kind]
+            copies.append(remote(ref.at[src_slot], ref.at[dst_slot], small_send.at[which, kind], small_recv.at[which, kind], peer))
+        return copies
 
     def send_small(*which):
         for kind in which:
@@ -154,9 +154,12 @@
             for copy in small_copies(kind):
                 copy.wait_recv()
 
-    for load in loads:
+    for load in loads[:2]:
         load.wait()
-    send(0, 0, 2, 1, 3, 4)
+    send(0, 0)
+    loads[2].wait()
+    send(0, 2, 1, 3, 4)
+    loads[3].start()
 
     @pl.when(colour == 1)
     def _():
@@ -191,6 +194,7 @@
     shifts[0].wait_recv()
     shifts[1].wait_recv()
     send_small(2, 0, 1)
+    loads[3].wait()
     send(1, 0, 2, 1, 3, 4)
     for slot in range(8):
         gate_own[slot] = gate_columns(OWN, expert_at(slot))
@@ -286,10 +290,9 @@
     prepare(OPP)
     arrive(1, 13, 14, 15, 16)
     prepare(OPP_SIB)
-    arrive(2, 5, 7)
-    send(2, 13, 15)
-    arrive(2, 6, 8)
-    send(2, 14, 16)
+    for piece in range(4):
+        arrive(2, (5, 7, 6, 8)[piece])
+        send(2, (13, 15, 14, 16)[piece])
     expert_rows(OPP, pl.ds(0, tokens), (u_opp[0], dh_opp[0]))
     arrive(2, 13, 14, 15, 16)
     expert_rows(OPP_SIB, pl.ds(0, tokens), (u_opp[1], dh_opp[1]))

time: 88.6 us -> 88.1 us (level)
  no operation moved by 1% of the time
where the time goes in v4:
time: 88.1 us; the launch traced here: 88 us
  Pallas kernels  87.4 us (99%)
    pallas_call x1, Pallas kernels, device_step(): pl.pallas_call(functools.partial(moe_kernel, stages, groups), name='moe',...  86 us

profile of v4, /device:TPU:1, one launch (start us, length us, event | category | flops | bytes accessed | tf_op | source)
XLA Modules:
  0.0 88.0 jit_solution(1944274787988354941)
XLA Ops:
  0.6 86.0 %moe.1 = (bf16[768,512]{1,0:T(8,128)(2,1)S(1)}, bf16[768,512]{1,0:T(8,128)(2,1)S(1)}, bf16[512,256]{1,0:T(8,128)(2,1)S(1)}, bf16[512,256]{1,0:T(8,128)(2,1)S(1)}, bf16[256,512]{1,0:T(8,128)(2,1)S(1)}) custom-call(bf16[768,512]{1,0:T(8,128)(2,1)} %bitcast.16, s32[2,768]{1,0:T(2,128)} %bitcast.21, f32[2,768]{1,0:T(2,128)} %bitcast.22, ...), custom_call_target="tpu_custom_call" | custom-call | tf_op jit(solution)/shard_map/moe/pallas_call | solution.py:329
  86.6 1.4 %finish.1 = (bf16[768,512]{1,0:T(8,128)(2,1)}, bf16[768,512]{1,0:T(8,128)(2,1)}, bf16[512,256]{1,0:T(8,128)(2,1)}, bf16[512,256]{1,0:T(8,128)(2,1)}, bf16[256,512]{1,0:T(8,128)(2,1)}) custom-call(bf16[768,512]{1,0:T(8,128)(2,1)S(1)} %get-tuple-element.15.refs_0_, bf16[768,512]{1,0:T(8,128)(2,1)S(1)} %get-tuple-element.16.refs_1_, ...), custom_call_target="tpu_custom_call" | custom-call | tf_op jit(solution)/shard_map/finish/pallas_call | solution.py:370

commit v5 on v4

--- a/solution.py
+++ b/solution.py
@@ -69,13 +69,18 @@
     after = {"stage": lax.rem(stage + 1, stages)}
     before = {"stage": lax.rem(stage + stages - 1, stages)}
 
+    def load_rows(src, row, rows, col, sem):
+        return pltpu.make_async_copy(src.at[pl.ds(row, rows)], w_all.at[OWN, pl.ds(row, rows), pl.ds(col, ff)], load_sem.at[sem])
+
     loads = [
-        pltpu.make_async_copy(up_hbm, w_all.at[OWN, pl.ds(0, d_model), pl.ds(0, ff)], load_sem.at[0]),
-        pltpu.make_async_copy(lin_hbm, w_all.at[OWN, pl.ds(0, d_model), pl.ds(ff, ff)], load_sem.at[1]),
-        pltpu.make_async_copy(down_hbm, w_all.at[OWN, pl.ds(d_model, ff)], load_sem.at[2]),
-        pltpu.make_async_copy(dy_hbm, d_all.at[OWN], load_sem.at[3]),
+        load_rows(up_hbm, 0, half, 0, 0),
+        load_rows(lin_hbm, 0, half, ff, 1),
+        load_rows(up_hbm, half, d_model - half, 0, 2),
+        load_rows(lin_hbm, half, d_model - half, ff, 3),
+        pltpu.make_async_copy(down_hbm, w_all.at[OWN, pl.ds(d_model, ff)], load_sem.at[4]),
+        pltpu.make_async_copy(dy_hbm, d_all.at[OWN], load_sem.at[5]),
     ]
-    for load in loads[:3]:
+    for load in loads[:5]:
         load.start()
 
     barrier = pltpu.get_barrier_semaphore()
@@ -157,9 +162,10 @@
     for load in loads[:2]:
         load.wait()
     send(0, 0)
-    loads[2].wait()
+    for load in loads[2:5]:
+        load.wait()
     send(0, 2, 1, 3, 4)
-    loads[3].start()
+    loads[5].start()
 
     @pl.when(colour == 1)
     def _():
@@ -194,7 +200,7 @@
     shifts[0].wait_recv()
     shifts[1].wait_recv()
     send_small(2, 0, 1)
-    loads[3].wait()
+    loads[5].wait()
     send(1, 0, 2, 1, 3, 4)
     for slot in range(8):
         gate_own[slot] = gate_columns(OWN, expert_at(slot))
@@ -353,7 +359,7 @@
                 pltpu.VMEM((ff, d_model), F32),
                 pltpu.VMEM((2, tokens, d_model), BF16),
                 pltpu.VMEM((2, tokens, ff), BF16),
-                dma((4,)),
+                dma((6,)),
                 dma((3, 17)),
                 dma((3, 17)),
                 dma((2, 7)),

time: 88.1 us -> 88.1 us (level)
  no operation moved by 1% of the time
where the time goes in v5:
time: 88.1 us; the launch traced here: 88 us
  Pallas kernels  87.4 us (99%)
    pallas_call x1, Pallas kernels, device_step(): pl.pallas_call(functools.partial(moe_kernel, stages, groups), name='moe',...  86 us

profile of v5, /device:TPU:1, one launch (start us, length us, event | category | flops | bytes accessed | tf_op | source)
XLA Modules:
  0.0 88.0 jit_solution(4196501882796016031)
XLA Ops:
  0.6 86.0 %moe.1 = (bf16[768,512]{1,0:T(8,128)(2,1)S(1)}, bf16[768,512]{1,0:T(8,128)(2,1)S(1)}, bf16[512,256]{1,0:T(8,128)(2,1)S(1)}, bf16[512,256]{1,0:T(8,128)(2,1)S(1)}, bf16[256,512]{1,0:T(8,128)(2,1)S(1)}) custom-call(bf16[768,512]{1,0:T(8,128)(2,1)} %bitcast.16, s32[2,768]{1,0:T(2,128)} %bitcast.21, f32[2,768]{1,0:T(2,128)} %bitcast.22, ...), custom_call_target="tpu_custom_call" | custom-call | tf_op jit(solution)/shard_map/moe/pallas_call | solution.py:335
  86.6 1.4 %finish.1 = (bf16[768,512]{1,0:T(8,128)(2,1)}, bf16[768,512]{1,0:T(8,128)(2,1)}, bf16[512,256]{1,0:T(8,128)(2,1)}, bf16[512,256]{1,0:T(8,128)(2,1)}, bf16[256,512]{1,0:T(8,128)(2,1)}) custom-call(bf16[768,512]{1,0:T(8,128)(2,1)S(1)} %get-tuple-element.15.refs_0_, bf16[768,512]{1,0:T(8,128)(2,1)S(1)} %get-tuple-element.16.refs_1_, ...), custom_call_target="tpu_custom_call" | custom-call | tf_op jit(solution)/shard_map/finish/pallas_call | solution.py:376
